TPU v7x, 32 devices: a whole 2x2x4 slice. The times are simulated.
32 devices in a mesh: rep: 2 (over y), grp: 4 (over z), tp: 2 (over x), sub: 2 (over core).
Axes of the slice: x: 2, y: 2, z: 4, core: 2. Of those that a mesh axis runs over, the one named last changes fastest.
Arguments:
- new_q: bfloat16 [4096, 8192], P(('rep', 'grp', 'sub'), 'tp'), parts along dimension 0
- new_kv: bfloat16 [2, 4096, 1024], P(None, ('rep', 'grp', 'sub'), 'tp'), parts along dimension 1
- hist_kv: bfloat16 [2, 8, 4, 4, 128, 1024], P(None, ('rep', 'grp'), None, None, 'sub', 'tp'), parts along dimension 1, may hold values from -6 to 6
- page_place: int32 [8, 16], P(('rep', 'grp')), parts along dimension 0, may hold values from 0 to 15, each once within a row
- hist_len: int32 [8], P(('rep', 'grp')), parts along dimension 0, may hold values from 1 to 2048, 4096 in all
- new_len: int32 [8], P(('rep', 'grp')), parts along dimension 0, may hold values from 128 to 512, as said below
- dec_q: bfloat16 [128, 8192], P(('rep', 'grp', 'sub'), 'tp'), parts along dimension 0
- dec_cache: bfloat16 [2, 128, 512, 1024], P(None, ('rep', 'grp', 'sub'), None, 'tp'), parts along dimension 1
- dec_len: int32 [128], P(('rep', 'grp', 'sub')), parts along dimension 0, may hold values from 64 to 512, as said below
Outputs:
- prefill_out: bfloat16 [4096, 8192], P(('rep', 'grp', 'sub'), 'tp'), parts along dimension 0
- decode_out: bfloat16 [128, 8192], P(('rep', 'grp', 'sub'), 'tp'), parts along dimension 0
There are 2 independent parts, one for each index of `rep`. A program takes and returns all parts, laid end to end along the dimension named above; each array names one. Nothing has to cross between parts.
Inputs may be any that keep to these rules, and one draw needn't show every extreme that they name: `page_place`: each row is an ordering of the slots 0 to 15: each owner holds exactly 4 pages of every conversation. `hist_len`: some conversation has exactly 2048. `new_len`: some conversation has exactly 512. `dec_len`: some request has exactly 512.
All inputs are finite; a program needn't handle non-finite values. No bound on the sum of `hist_len` on one device may be relied on, other than what follows from the above.
Results may differ from a plain program's by a relative error of at most 0.008.
Values may be sent and summed in bfloat16 or wider, within the bound.
No kernel may reach another device: no remote copies, remote signals or barrier semaphores. Data moves between devices by JAX's collectives and lax.ppermute only.
A program may use at most 128 MiB of HBM per device.

v0:
```python
import functools
import math

import jax
import jax.numpy as jnp
from jax import lax
from jax.experimental import pallas as pl
from jax.experimental.pallas import tpu as pltpu
from jax.sharding import PartitionSpec as P

HQ = 64
KVH = 8
HD = 128
PAGE = 128
GROUP = HQ // KVH
NEG = -1e30
COEF = (HD**-0.5) * math.log2(math.e)


def dot_t(a, b):
    return lax.dot_general(a, b, (((1,), (1,)), ((), ())), preferred_element_type=jnp.float32)


def dot_n(a, b):
    return lax.dot_general(a, b, (((1,), (0,)), ((), ())), preferred_element_type=jnp.float32)


def local_kernel(info, q_ref, *refs, parts):
    kv_refs, (acc_out, ml_out) = refs[:parts], refs[parts:]
    rows = q_ref.shape[0]
    q_base, count = info[0], info[1]
    keys = jnp.concatenate([r[0] for r in kv_refs], axis=0)
    values = jnp.concatenate([r[1] for r in kv_refs], axis=0)
    q_pos = q_base + lax.broadcasted_iota(jnp.int32, (rows, rows), 0)
    biases = []
    for p in range(parts):
        k_pos = info[2 + p] + lax.broadcasted_iota(jnp.int32, (rows, rows), 1)
        biases.append(jnp.where((k_pos <= q_pos) & (k_pos < count), 0.0, NEG))
    bias = jnp.concatenate(biases, axis=1)
    lane = lax.broadcasted_iota(jnp.int32, (rows, HD), 1)
    ml = jnp.zeros((rows, HD), jnp.float32)
    for h in range(GROUP):
        cols = slice(h * HD, (h + 1) * HD)
        scores = dot_t(q_ref[:, cols], keys) * COEF + bias
        top = jnp.max(scores, axis=1, keepdims=True)
        weights = jnp.exp2(scores - top)
        total = jnp.sum(weights, axis=1, keepdims=True)
        acc_out[:, cols] = dot_n(weights.astype(jnp.bfloat16), values)
        ml = jnp.where(lane == h, top, ml)
        ml = jnp.where(lane == GROUP + h, total, ml)
    ml_out[0] = ml


def page_kernel(info, q_ref, *refs, parts, offset, last):
    kv_refs, (acc_in, ml_in), outs = refs[:parts], refs[parts : parts + 2], refs[parts + 2 :]
    rows = q_ref.shape[0]
    slots, tokens = kv_refs[0].shape[1], kv_refs[0].shape[2]
    total_keys = parts * slots * tokens
    base = 2 + parts + offset * parts * slots
    counts = [info[base + i] for i in range(parts * slots)]
    any_keys = functools.reduce(jnp.add, counts) > 0

    def write(cols, acc, total):
        q_pos = info[0] + lax.broadcasted_iota(jnp.int32, (rows, HD), 0)
        outs[0][:, cols] = jnp.where(q_pos < info[1], acc / total, 0.0).astype(jnp.bfloat16)

    @pl.when(any_keys)
    def _():
        keys = jnp.concatenate([r[0].reshape(slots * tokens, HD) for r in kv_refs], axis=0)
        values = jnp.concatenate([r[1].reshape(slots * tokens, HD) for r in kv_refs], axis=0)
        token = lax.broadcasted_iota(jnp.int32, (1, total_keys), 1)
        limit = jnp.zeros((1, total_keys), jnp.int32)
        for i, c in enumerate(counts):
            limit = jnp.where(token >= i * tokens, i * tokens + c, limit)
        bias = jnp.where(token < limit, 0.0, NEG)
        lane = lax.broadcasted_iota(jnp.int32, (rows, HD), 1)
        ml_old = ml_in[0]
        ml = ml_old
        for h in range(GROUP):
            cols = slice(h * HD, (h + 1) * HD)
            scores = dot_t(q_ref[:, cols], keys) * COEF + bias
            old = ml_old[:, h : h + 1]
            top = jnp.maximum(old, jnp.max(scores, axis=1, keepdims=True))
            weights = jnp.exp2(scores - top)
            factor = jnp.exp2(old - top)
            total = ml_old[:, GROUP + h : GROUP + h + 1] * factor + jnp.sum(
                weights, axis=1, keepdims=True
            )
            acc = acc_in[:, cols] * factor + dot_n(weights.astype(jnp.bfloat16), values)
            if last:
                write(cols, acc, total)
            else:
                outs[0][:, cols] = acc
                ml = jnp.where(lane == h, top, ml)
                ml = jnp.where(lane == GROUP + h, total, ml)
        if not last:
            outs[1][0] = ml

    @pl.when(jnp.logical_not(any_keys))
    def _():
        for h in range(GROUP):
            cols = slice(h * HD, (h + 1) * HD)
            if last:
                write(cols, acc_in[:, cols], ml_in[0][:, GROUP + h : GROUP + h + 1])
            else:
                outs[0][:, cols] = acc_in[:, cols]
        if not last:
            outs[1][0] = ml_in[0]


def decode_kernel(lens, q_ref, kv_ref, out_ref):
    r = pl.program_id(0)
    cached = kv_ref.shape[2]
    token = lax.broadcasted_iota(jnp.int32, (1, cached), 1)
    bias = jnp.where(token < lens[r], 0.0, NEG)
    for k in range(kv_ref.shape[3] // HD):
        cols = slice(k * HD, (k + 1) * HD)
        heads = slice(k * GROUP, (k + 1) * GROUP)
        scores = dot_t(q_ref[0, heads, :], kv_ref[0, 0, :, cols]) * COEF + bias
        top = jnp.max(scores, axis=1, keepdims=True)
        weights = jnp.exp2(scores - top)
        total = jnp.sum(weights, axis=1, keepdims=True)
        mixed = dot_n(weights.astype(jnp.bfloat16), kv_ref[1, 0, :, cols])
        out_ref[0, heads, :] = (mixed / total).astype(jnp.bfloat16)


def cost(rows, heads, keys, nbytes):
    return pl.CostEstimate(
        flops=4 * rows * heads * keys * HD, transcendentals=rows * heads * keys, bytes_accessed=nbytes
    )


def run_local(info, q, kvs):
    rows = q.shape[0]
    kv_local = kvs[0].shape[2] // HD
    wide = GROUP * HD
    return pl.pallas_call(
        functools.partial(local_kernel, parts=len(kvs)),
        grid_spec=pltpu.PrefetchScalarGridSpec(
            num_scalar_prefetch=1,
            grid=(kv_local,),
            in_specs=[pl.BlockSpec((rows, wide), lambda k, s: (0, k))]
            + [pl.BlockSpec((2, rows, HD), lambda k, s: (0, 0, k)) for _ in kvs],
            out_specs=[
                pl.BlockSpec((rows, wide), lambda k, s: (0, k)),
                pl.BlockSpec((1, rows, HD), lambda k, s: (k, 0, 0)),
            ],
        ),
        out_shape=[
            jax.ShapeDtypeStruct((rows, kv_local * wide), jnp.float32),
            jax.ShapeDtypeStruct((kv_local, rows, HD), jnp.float32),
        ],
        cost_estimate=cost(rows, kv_local * GROUP, rows * len(kvs), rows * kv_local * wide * 6),
        name="local_stage",
    )(info, q, *kvs)


def run_pages(info, q, kvs, acc, ml, offset, last):
    rows = q.shape[0]
    slots, tokens = kvs[0].shape[1], kvs[0].shape[2]
    kv_local = kvs[0].shape[3] // HD
    wide = GROUP * HD
    acc_spec = pl.BlockSpec((rows, wide), lambda k, s: (0, k))
    ml_spec = pl.BlockSpec((1, rows, HD), lambda k, s: (k, 0, 0))
    parts = len(kvs)
    if last:
        out_specs = [acc_spec]
        out_shape = [jax.ShapeDtypeStruct(acc.shape, jnp.bfloat16)]
        aliases = {}
    else:
        out_specs = [acc_spec, ml_spec]
        out_shape = [
            jax.ShapeDtypeStruct(acc.shape, jnp.float32),
            jax.ShapeDtypeStruct(ml.shape, jnp.float32),
        ]
        aliases = {2 + parts: 0, 3 + parts: 1}
    return pl.pallas_call(
        functools.partial(page_kernel, parts=parts, offset=offset, last=last),
        grid_spec=pltpu.PrefetchScalarGridSpec(
            num_scalar_prefetch=1,
            grid=(kv_local,),
            in_specs=[pl.BlockSpec((rows, wide), lambda k, s: (0, k))]
            + [pl.BlockSpec((2, slots, tokens, HD), lambda k, s: (0, 0, 0, k)) for _ in kvs]
            + [acc_spec, ml_spec],
            out_specs=out_specs,
        ),
        out_shape=out_shape,
        input_output_aliases=aliases,
        cost_estimate=cost(
            rows, kv_local * GROUP, parts * slots * tokens, rows * kv_local * wide * 10
        ),
        name="page_stage_last" if last else "page_stage",
    )(info, q, *kvs, acc, ml)


def run_decode(dec_q, dec_cache, dec_len):
    requests, width = dec_q.shape
    heads = width // HD
    cached, kv_width = dec_cache.shape[2], dec_cache.shape[3]
    out = pl.pallas_call(
        decode_kernel,
        grid_spec=pltpu.PrefetchScalarGridSpec(
            num_scalar_prefetch=1,
            grid=(requests,),
            in_specs=[
                pl.BlockSpec((1, heads, HD), lambda r, s: (r, 0, 0)),
                pl.BlockSpec((2, 1, cached, kv_width), lambda r, s: (0, r, 0, 0)),
            ],
            out_specs=pl.BlockSpec((1, heads, HD), lambda r, s: (r, 0, 0)),
        ),
        out_shape=jax.ShapeDtypeStruct((requests, heads, HD), jnp.bfloat16),
        cost_estimate=cost(requests, heads, cached, 2 * dec_cache.size),
        name="decode_stage",
    )(dec_len, dec_q.reshape(requests, heads, HD), dec_cache)
    return out.reshape(requests, width)


def shift(block, axis, distance):
    size = lax.axis_size(axis)
    return lax.ppermute(block, axis, [(i, (i + distance) % size) for i in range(size)])


def attend(new_q, new_kv, hist_kv, page_place, hist_len, new_len, dec_q, dec_cache, dec_len):
    rows = new_q.shape[0]
    owners, subs = lax.axis_size("grp"), lax.axis_size("sub")
    own, sub = lax.axis_index("grp"), lax.axis_index("sub")
    slots, tokens = hist_kv.shape[3], hist_kv.shape[4]

    order = sorted(range(1, owners), key=lambda k: (-min(k, owners - k), k))
    arrived = {}
    for k in order:
        dest = lax.rem(own + k, owners)
        piece = lax.dynamic_slice_in_dim(hist_kv, dest, 1, 2)[:, 0, 0]
        arrived[k] = shift(piece, "grp", k)
    arrived[0] = lax.dynamic_slice_in_dim(hist_kv, own, 1, 2)[:, 0, 0]

    i32 = jnp.int32
    place = page_place[0]
    slot_id = lax.rem(own - jnp.arange(owners, dtype=i32) + owners, owners)[:, None] * slots
    slot_id = slot_id + jnp.arange(slots, dtype=i32)[None, :]
    page = jnp.sum(
        jnp.where(
            place[None, None, :] == slot_id[:, :, None],
            jnp.arange(place.shape[0], dtype=i32)[None, None, :],
            0,
        ),
        axis=2,
    )
    half = lax.rem(sub - jnp.arange(subs, dtype=i32) + subs, subs)
    start = page[:, None, :] * PAGE + half[None, :, None] * tokens
    visible = jnp.clip(hist_len[0] - start, 0, tokens)
    info = jnp.concatenate(
        [(sub * rows).reshape(1), new_len, half * rows, visible.reshape(-1)]
    ).astype(i32)

    def both(block):
        return [block] + [shift(block, "sub", s) for s in range(1, subs)]

    decode_out = run_decode(dec_q, dec_cache, dec_len)
    acc, ml = run_local(info, new_q, both(new_kv))
    stages = [0] + order
    for k in stages:
        last = k == stages[-1]
        block = arrived[k]
        if k:
            block, ml, decode_out = lax.optimization_barrier((block, ml, decode_out))
        found = run_pages(info, new_q, both(block), acc, ml, k, last)
        if last:
            prefill_out = found[0]
        else:
            acc, ml = found
    return (prefill_out, decode_out)


def solution(mesh):
    in_specs = (
        P(("rep", "grp", "sub"), "tp"),
        P(None, ("rep", "grp", "sub"), "tp"),
        P(None, ("rep", "grp"), None, None, "sub", "tp"),
        P(("rep", "grp"), None),
        P(("rep", "grp")),
        P(("rep", "grp")),
        P(("rep", "grp", "sub"), "tp"),
        P(None, ("rep", "grp", "sub"), None, "tp"),
        P(("rep", "grp", "sub")),
    )
    out_specs = (P(("rep", "grp", "sub"), "tp"), P(("rep", "grp", "sub"), "tp"))
    return jax.shard_map(attend, mesh=mesh, in_specs=in_specs, out_specs=out_specs, check_vma=False)
```

profile of v0, /device:TPU:0, one launch (start us, length us, event | category | flops | bytes accessed | tf_op | source)
XLA Modules:
  0.0 119.5 jit_solution(8321493333839715040)
XLA Ops:
  0.6 0.0 copy-start.5
  0.7 1.7 %dynamic-slice_bitcast_fusion = (bf16[2,4,64,512]{3,2,1,0:T(8,128)(2,1)S(1)}, bf16[2,4,64,512]{3,2,1,0:T(8,128)(2,1)S(1)}, bf16[2,4,64,512]{3,2,1,0:T(8,128)(2,1)S(1)}, bf16[2,4,64,512]{3,2,1,0:T(8,128)(2,1)S(1)}) fusion(bf16[2,1,4,4,64,512]{5,4,3,2,1,0:T(8,128)(2,1)} %param.11, s32[]{:T(128)S(6)} %select_n.20, s32[]{:T(128)S(6)} %select_n.18, ...), kind=kLoop, calls=%fused_computation | loop fusion | bytes 4194320 | tf_op jit(solution)/shard_map/squeeze | solution.py:235
  2.4 0.0 copy-start.2
  2.4 4.1 %collective-permute-start.2 = (bf16[2,4,64,512]{3,2,1,0:T(8,128)(2,1)S(1)}, bf16[2,4,64,512]{3,2,1,0:T(8,128)(2,1)S(1)}, u32[]{:S(2)}, u32[]{:S(2)}) collective-permute-start(bf16[2,4,64,512]{3,2,1,0:T(8,128)(2,1)S(1)} %get-tuple-element.39), channel_id=1, source_target_pairs={{0,8},{4,12},{8,0},{12,4},{1,9},{5,13},{9,1},{13,5},{2,10},{6,14},... | collective-permute-start | bytes 1572872 | tf_op jit(solution)/shard_map/ppermute | solution.py:220
  6.6 0.0 collective-permute-start.3
  6.6 0.5 collective-permute-start.4
  7.1 0.1 iota_add_fusion
  7.2 0.2 select_reduce_fusion
  8.1 0.1 subtract_clamp_fusion
  8.2 0.1 min.12
  8.9 0.6 copy.22
  9.6 11.7 %decode_stage.1 = bf16[8,32,128]{2,1,0:T(8,128)(2,1)} custom-call(s32[8]{0:T(128)} %lens.1, bf16[8,32,128]{2,1,0:T(8,128)(2,1)} %bitcast.21, bf16[2,8,512,512]{3,2,1,0:T(8,128)(2,1)} %kv_ref.1), custom_call_target="tpu_custom_call" | custom-call | flops 67108864 | bytes 8388608 | tf_op jit(solution)/shard_map/decode_stage/pallas_call | solution.py:200
  21.2 1.5 %copy.21 = bf16[1,8,32,128]{3,1,2,0:T(8,128)(2,1)} copy(bf16[1,8,32,128]{3,2,1,0:T(8,128)(2,1)} %bitcast.20) | data formatting | bytes 131072
  22.7 0.6 pad_add_fusion.info
  23.4 0.0 collective-permute-done.4.refs_1_
  23.4 13.2 %local_stage.1 = (f32[256,4096]{1,0:T(8,128)}, f32[4,256,128]{2,1,0:T(8,128)}) custom-call(s32[36]{0:T(128)} %pad_add_fusion.info, bf16[256,4096]{1,0:T(8,128)(2,1)} %q_ref.9, bf16[2,256,512]{2,1,0:T(8,128)(2,1)} %refs_0_.1, bf16[2,256,512]{2,1,0:T(8,128)(2,1)} %collective-permute-done.4.refs_1_), custom_call_target="tpu_custom_call" | custom-call | flops 2147483648 | bytes 6291456 | tf_op jit(solution)/shard_map/local_stage/pallas_call | solution.py:137
  36.6 0.0 collective-permute-done.3.refs_1_
  36.6 18.4 %page_stage.3 = (f32[256,4096]{1,0:T(8,128)}, f32[4,256,128]{2,1,0:T(8,128)}) custom-call(s32[36]{0:T(128)} %pad_add_fusion.info, bf16[256,4096]{1,0:T(8,128)(2,1)} %q_ref.9, bf16[2,4,64,512]{3,2,1,0:T(8,128)(2,1)} %copy-done.2, bf16[2,4,64,512]{3,2,1,0:T(8,128)(2,1)} %collective-permute-done.3.refs_1_, ...), custom_call_target="tpu_custom_call", output_to_operand_aliasing={{0}: (4, {}), {1}: (5, {})} | custom-call | flops 2147483648 | bytes 10485760 | tf_op jit(solution)/shard_map/page_stage/pallas_call | solution.py:177
  55.1 0.1 collective-permute-start.5
  55.2 0.0 collective-permute-start.1
  55.2 1.8 %collective-permute-done.5.refs_1_ = bf16[2,4,64,512]{3,2,1,0:T(8,128)(2,1)S(1)} collective-permute-done((bf16[2,4,64,512]{3,2,1,0:T(8,128)(2,1)S(1)}, bf16[2,4,64,512]{3,2,1,0:T(8,128)(2,1)S(1)}, u32[]{:S(2)}, u32[]{:S(2)}) %collective-permute-start.5) | collective-permute-done | bytes 524320 | tf_op jit(solution)/shard_map/ppermute | solution.py:220
  57.1 0.8 copy-done.9
  57.9 18.4 %page_stage.4 = (f32[256,4096]{1,0:T(8,128)}, f32[4,256,128]{2,1,0:T(8,128)}) custom-call(s32[36]{0:T(128)} %pad_add_fusion.info, bf16[256,4096]{1,0:T(8,128)(2,1)} %q_ref.9, bf16[2,4,64,512]{3,2,1,0:T(8,128)(2,1)} %copy-done.6, bf16[2,4,64,512]{3,2,1,0:T(8,128)(2,1)} %copy-done.9, ...), custom_call_target="tpu_custom_call", output_to_operand_aliasing={{0}: (4, {}), {1}: (5, {})} | custom-call | flops 2147483648 | bytes 10485760 | tf_op jit(solution)/shard_map/page_stage/pallas_call | solution.py:177
  76.3 0.0 collective-permute-done.1.refs_0_
  76.3 0.2 collective-permute-start.6
  76.5 2.1 %collective-permute-start = (bf16[2,4,64,512]{3,2,1,0:T(8,128)(2,1)S(1)}, bf16[2,4,64,512]{3,2,1,0:T(8,128)(2,1)S(1)}, u32[]{:S(2)}, u32[]{:S(2)}) collective-permute-start(bf16[2,4,64,512]{3,2,1,0:T(8,128)(2,1)S(1)} %get-tuple-element.38), channel_id=1, source_target_pairs={{0,12},{4,0},{8,4},{12,8},{1,13},{5,1},{9,5},{13,9},{2,14},{6,2},{... | collective-permute-start | bytes 1572872 | tf_op jit(solution)/shard_map/ppermute | solution.py:220
  78.6 0.8 copy-done.8
  79.4 18.4 %page_stage.5 = (f32[256,4096]{1,0:T(8,128)}, f32[4,256,128]{2,1,0:T(8,128)}) custom-call(s32[36]{0:T(128)} %pad_add_fusion.info, bf16[256,4096]{1,0:T(8,128)(2,1)} %q_ref.9, bf16[2,4,64,512]{3,2,1,0:T(8,128)(2,1)} %copy-done.7, bf16[2,4,64,512]{3,2,1,0:T(8,128)(2,1)} %copy-done.8, ...), custom_call_target="tpu_custom_call", output_to_operand_aliasing={{0}: (4, {}), {1}: (5, {})} | custom-call | flops 2147483648 | bytes 10485760 | tf_op jit(solution)/shard_map/page_stage/pallas_call | solution.py:177
  97.9 0.1 collective-permute-start.7
  97.9 1.9 %collective-permute-done.7.refs_1_ = bf16[2,4,64,512]{3,2,1,0:T(8,128)(2,1)S(1)} collective-permute-done((bf16[2,4,64,512]{3,2,1,0:T(8,128)(2,1)S(1)}, bf16[2,4,64,512]{3,2,1,0:T(8,128)(2,1)S(1)}, u32[]{:S(2)}, u32[]{:S(2)}) %collective-permute-start.7) | collective-permute-done | bytes 524320 | tf_op jit(solution)/shard_map/ppermute | solution.py:220
  99.8 0.8 copy-done.1
  100.6 18.8 %page_stage_last.1 = bf16[256,4096]{1,0:T(8,128)(2,1)} custom-call(s32[36]{0:T(128)} %pad_add_fusion.info, bf16[256,4096]{1,0:T(8,128)(2,1)} %q_ref.9, bf16[2,4,64,512]{3,2,1,0:T(8,128)(2,1)} %copy-done, bf16[2,4,64,512]{3,2,1,0:T(8,128)(2,1)} %copy-done.1, f32[256,4096]{1,0:T(8,128)} %get-tuple-element.33.refs_2_, f32[4,256,128]{2,1,0:T(8,128)} %get-tuple-element.34.refs_3_), custom_call_target="tpu_custom_call" | custom-call | flops 2147483648 | bytes 10485760 | tf_op jit(solution)/shard_map/page_stage_last/pallas_call | solution.py:177
  (22 shorter events, 0.1 us)
Async XLA Ops:
  0.6 6.0 %copy-start.5 = (bf16[2,256,512]{2,1,0:T(8,128)(2,1)S(1)}, bf16[2,256,512]{2,1,0:T(8,128)(2,1)}, u32[]{:S(2)}) copy-start(bf16[2,256,512]{2,1,0:T(8,128)(2,1)} %refs_0_.1) | copy-start | bytes 1572868
  0.6 6.5 %copy-start.4 = (s32[1,16]{1,0:T(1,128)S(1)}, s32[1,16]{1,0:T(1,128)}, u32[]{:S(2)}) copy-start(s32[1,16]{1,0:T(1,128)} %param.12) | copy-start | bytes 196
  0.7 8.3 %copy-start.3 = (bf16[8,4096]{1,0:T(8,128)(2,1)S(1)}, bf16[8,4096]{1,0:T(8,128)(2,1)}, u32[]{:S(2)}) copy-start(bf16[8,4096]{1,0:T(8,128)(2,1)} %param.15) | copy-start | bytes 196612
  2.4 18.8 %copy-start.2 = (bf16[2,4,64,512]{3,2,1,0:T(8,128)(2,1)}, bf16[2,4,64,512]{3,2,1,0:T(8,128)(2,1)S(1)}, u32[]{:S(2)}) copy-start(bf16[2,4,64,512]{3,2,1,0:T(8,128)(2,1)S(1)} %get-tuple-element.36.refs_0_) | copy-start | bytes 1572868
  2.4 52.6 %collective-permute-start.2 = (bf16[2,4,64,512]{3,2,1,0:T(8,128)(2,1)S(1)}, bf16[2,4,64,512]{3,2,1,0:T(8,128)(2,1)S(1)}, u32[]{:S(2)}, u32[]{:S(2)}) collective-permute-start(bf16[2,4,64,512]{3,2,1,0:T(8,128)(2,1)S(1)} %get-tuple-element.39), channel_id=1, source_target_pairs={{0,8},{4,12},{8,0},{12,4},{1,9},{5,13},{9,1},{13,5},{2,10},{6,14},... | collective-permute-start | bytes 1572872 | tf_op jit(solution)/shard_map/ppermute | solution.py:220
  6.6 30.0 %collective-permute-start.3 = (bf16[2,4,64,512]{3,2,1,0:T(8,128)(2,1)S(1)}, bf16[2,4,64,512]{3,2,1,0:T(8,128)(2,1)}, u32[]{:S(2)}, u32[]{:S(2)}) collective-permute-start(bf16[2,4,64,512]{3,2,1,0:T(8,128)(2,1)S(1)} %get-tuple-element.36.refs_0_), channel_id=1, source_target_pairs={{0,1},{1,0},{2,3},{3,2},{4,5},{5,4},{6,7},{7,6},{8,9},{9,8},{10,11... | collective-permute-start | bytes 1572872 | tf_op jit(solution)/shard_map/ppermute | solution.py:220
  6.6 16.8 %collective-permute-start.4 = (bf16[2,256,512]{2,1,0:T(8,128)(2,1)S(1)}, bf16[2,256,512]{2,1,0:T(8,128)(2,1)}, u32[]{:S(2)}, u32[]{:S(2)}) collective-permute-start(bf16[2,256,512]{2,1,0:T(8,128)(2,1)S(1)} %copy-done.5), channel_id=1, source_target_pairs={{0,1},{1,0},{2,3},{3,2},{4,5},{5,4},{6,7},{7,6},{8,9},{9,8},{10,11... | collective-permute-start | bytes 1572872 | tf_op jit(solution)/shard_map/ppermute | solution.py:220
  55.1 2.0 %copy-start.6 = (bf16[2,4,64,512]{3,2,1,0:T(8,128)(2,1)}, bf16[2,4,64,512]{3,2,1,0:T(8,128)(2,1)S(1)}, u32[]{:S(2)}) copy-start(bf16[2,4,64,512]{3,2,1,0:T(8,128)(2,1)S(1)} %collective-permute-done.2.refs_0_) | copy-start | bytes 1572868
  55.1 2.0 %collective-permute-start.5 = (bf16[2,4,64,512]{3,2,1,0:T(8,128)(2,1)S(1)}, bf16[2,4,64,512]{3,2,1,0:T(8,128)(2,1)S(1)}, u32[]{:S(2)}, u32[]{:S(2)}) collective-permute-start(bf16[2,4,64,512]{3,2,1,0:T(8,128)(2,1)S(1)} %collective-permute-done.2.refs_0_), channel_id=1, source_target_pairs={{0,1},{1,0},{2,3},{3,2},{4,5},{5,4},{6,7},{7,6},{8,9},{9,8},{10,11... | collective-permute-start | bytes 1572872 | tf_op jit(solution)/shard_map/ppermute | solution.py:220
  55.2 21.1 %collective-permute-start.1 = (bf16[2,4,64,512]{3,2,1,0:T(8,128)(2,1)S(1)}, bf16[2,4,64,512]{3,2,1,0:T(8,128)(2,1)S(1)}, u32[]{:S(2)}, u32[]{:S(2)}) collective-permute-start(bf16[2,4,64,512]{3,2,1,0:T(8,128)(2,1)S(1)} %get-tuple-element.37), channel_id=1, source_target_pairs={{0,4},{4,8},{8,12},{12,0},{1,5},{5,9},{9,13},{13,1},{2,6},{6,10},{... | collective-permute-start | bytes 1572872 | tf_op jit(solution)/shard_map/ppermute | solution.py:220
  57.1 0.8 copy-start.9
  76.3 2.3 %copy-start.7 = (bf16[2,4,64,512]{3,2,1,0:T(8,128)(2,1)}, bf16[2,4,64,512]{3,2,1,0:T(8,128)(2,1)S(1)}, u32[]{:S(2)}) copy-start(bf16[2,4,64,512]{3,2,1,0:T(8,128)(2,1)S(1)} %collective-permute-done.1.refs_0_) | copy-start | bytes 1572868
  76.3 2.3 %collective-permute-start.6 = (bf16[2,4,64,512]{3,2,1,0:T(8,128)(2,1)S(1)}, bf16[2,4,64,512]{3,2,1,0:T(8,128)(2,1)S(1)}, u32[]{:S(2)}, u32[]{:S(2)}) collective-permute-start(bf16[2,4,64,512]{3,2,1,0:T(8,128)(2,1)S(1)} %collective-permute-done.1.refs_0_), channel_id=1, source_target_pairs={{0,1},{1,0},{2,3},{3,2},{4,5},{5,4},{6,7},{7,6},{8,9},{9,8},{10,11... | collective-permute-start | bytes 1572872 | tf_op jit(solution)/shard_map/ppermute | solution.py:220
  76.5 21.4 %collective-permute-start = (bf16[2,4,64,512]{3,2,1,0:T(8,128)(2,1)S(1)}, bf16[2,4,64,512]{3,2,1,0:T(8,128)(2,1)S(1)}, u32[]{:S(2)}, u32[]{:S(2)}) collective-permute-start(bf16[2,4,64,512]{3,2,1,0:T(8,128)(2,1)S(1)} %get-tuple-element.38), channel_id=1, source_target_pairs={{0,12},{4,0},{8,4},{12,8},{1,13},{5,1},{9,5},{13,9},{2,14},{6,2},{... | collective-permute-start | bytes 1572872 | tf_op jit(solution)/shard_map/ppermute | solution.py:220
  78.6 0.8 copy-start.8
  97.9 2.0 %copy-start = (bf16[2,4,64,512]{3,2,1,0:T(8,128)(2,1)}, bf16[2,4,64,512]{3,2,1,0:T(8,128)(2,1)S(1)}, u32[]{:S(2)}) copy-start(bf16[2,4,64,512]{3,2,1,0:T(8,128)(2,1)S(1)} %collective-permute-done.refs_0_) | copy-start | bytes 1572868
  97.9 2.0 %collective-permute-start.7 = (bf16[2,4,64,512]{3,2,1,0:T(8,128)(2,1)S(1)}, bf16[2,4,64,512]{3,2,1,0:T(8,128)(2,1)S(1)}, u32[]{:S(2)}, u32[]{:S(2)}) collective-permute-start(bf16[2,4,64,512]{3,2,1,0:T(8,128)(2,1)S(1)} %collective-permute-done.refs_0_), channel_id=1, source_target_pairs={{0,1},{1,0},{2,3},{3,2},{4,5},{5,4},{6,7},{7,6},{8,9},{9,8},{10,11... | collective-permute-start | bytes 1572872 | tf_op jit(solution)/shard_map/ppermute | solution.py:220
  99.8 0.8 copy-start.1
where the time goes:
time: 120 us; the launch traced here: 119 us
  Pallas kernels  99.1 us (83%)
  starting transfers between devices  7.13 us (6%)
  local copies, waits for them, and re-layouts  6.39 us (5%)
  waiting for transfers between devices  3.74 us (3%)
  between operations  2.08 us (2%)
    pallas_call x4, Pallas kernels, run_pages(): pl.pallas_call(functools.partial(page_kernel, parts=parts, offset=offset,...  74.2 us
    pallas_call x1, Pallas kernels, run_local(): pl.pallas_call(functools.partial(local_kernel, parts=len(kvs)), grid_spec...  13.2 us
    pallas_call x1, Pallas kernels, run_decode(): pl.pallas_call(decode_kernel, grid_spec=pltpu.PrefetchScalarGridSpec(num_...  11.7 us
    ppermute x8, starting transfers between devices, shift(): lax.ppermute(block, axis, [(i, (i + distance) % size) for i in range(size)])  7.13 us
    unnamed x22, local copies, waits for them, and re-layouts  4.56 us
    ppermute x8, waiting for transfers between devices, shift(): lax.ppermute(block, axis, [(i, (i + distance) % size) for i in range(size)])  3.74 us
  transfers between devices with their start and end apart: 8, of which 2 were waited for; matrix products, arithmetic and copies ran while one was open for 3% of the time, Pallas kernels for 67%

commit v1 on v0

--- a/solution.py
+++ b/solution.py
@@ -30,82 +30,76 @@
     rows = q_ref.shape[0]
     q_base, count = info[0], info[1]
     keys = jnp.concatenate([r[0] for r in kv_refs], axis=0)
-    values = jnp.concatenate([r[1] for r in kv_refs], axis=0)
-    q_pos = q_base + lax.broadcasted_iota(jnp.int32, (rows, rows), 0)
+    values = jnp.concatenate([r[1] for r in kv_refs], axis=0).T
+    q_pos = q_base + lax.broadcasted_iota(jnp.int32, (rows, rows), 1)
     biases = []
     for p in range(parts):
-        k_pos = info[2 + p] + lax.broadcasted_iota(jnp.int32, (rows, rows), 1)
+        k_pos = info[2 + p] + lax.broadcasted_iota(jnp.int32, (rows, rows), 0)
         biases.append(jnp.where((k_pos <= q_pos) & (k_pos < count), 0.0, NEG))
-    bias = jnp.concatenate(biases, axis=1)
-    lane = lax.broadcasted_iota(jnp.int32, (rows, HD), 1)
-    ml = jnp.zeros((rows, HD), jnp.float32)
+    bias = jnp.concatenate(biases, axis=0)
+    raw = dot_t(keys, q_ref[:, :HD])
     for h in range(GROUP):
         cols = slice(h * HD, (h + 1) * HD)
-        scores = dot_t(q_ref[:, cols], keys) * COEF + bias
-        top = jnp.max(scores, axis=1, keepdims=True)
+        scores = raw * COEF + bias
+        if h + 1 < GROUP:
+            raw = dot_t(keys, q_ref[:, (h + 1) * HD : (h + 2) * HD])
+        top = jnp.max(scores, axis=0, keepdims=True)
         weights = jnp.exp2(scores - top)
-        total = jnp.sum(weights, axis=1, keepdims=True)
-        acc_out[:, cols] = dot_n(weights.astype(jnp.bfloat16), values)
-        ml = jnp.where(lane == h, top, ml)
-        ml = jnp.where(lane == GROUP + h, total, ml)
-    ml_out[0] = ml
+        ml_out[0, h : h + 1, :] = top
+        ml_out[0, GROUP + h : GROUP + h + 1, :] = jnp.sum(weights, axis=0, keepdims=True)
+        acc_out[cols, :] = dot_n(values, weights.astype(jnp.bfloat16))
 
 
 def page_kernel(info, q_ref, *refs, parts, offset, last):
     kv_refs, (acc_in, ml_in), outs = refs[:parts], refs[parts : parts + 2], refs[parts + 2 :]
     rows = q_ref.shape[0]
     slots, tokens = kv_refs[0].shape[1], kv_refs[0].shape[2]
-    total_keys = parts * slots * tokens
     base = 2 + parts + offset * parts * slots
     counts = [info[base + i] for i in range(parts * slots)]
     any_keys = functools.reduce(jnp.add, counts) > 0
 
     def write(cols, acc, total):
         q_pos = info[0] + lax.broadcasted_iota(jnp.int32, (rows, HD), 0)
-        outs[0][:, cols] = jnp.where(q_pos < info[1], acc / total, 0.0).astype(jnp.bfloat16)
+        mixed = (acc / total).T
+        outs[0][:, cols] = jnp.where(q_pos < info[1], mixed, 0.0).astype(jnp.bfloat16)
 
     @pl.when(any_keys)
     def _():
         keys = jnp.concatenate([r[0].reshape(slots * tokens, HD) for r in kv_refs], axis=0)
-        values = jnp.concatenate([r[1].reshape(slots * tokens, HD) for r in kv_refs], axis=0)
-        token = lax.broadcasted_iota(jnp.int32, (1, total_keys), 1)
-        limit = jnp.zeros((1, total_keys), jnp.int32)
-        for i, c in enumerate(counts):
-            limit = jnp.where(token >= i * tokens, i * tokens + c, limit)
-        bias = jnp.where(token < limit, 0.0, NEG)
-        lane = lax.broadcasted_iota(jnp.int32, (rows, HD), 1)
-        ml_old = ml_in[0]
-        ml = ml_old
+        values = jnp.concatenate([r[1].reshape(slots * tokens, HD) for r in kv_refs], axis=0).T
+        token = lax.broadcasted_iota(jnp.int32, (tokens, rows), 0)
+        bias = jnp.concatenate([jnp.where(token < c, 0.0, NEG) for c in counts], axis=0)
+        raw = dot_t(keys, q_ref[:, :HD])
         for h in range(GROUP):
             cols = slice(h * HD, (h + 1) * HD)
-            scores = dot_t(q_ref[:, cols], keys) * COEF + bias
-            old = ml_old[:, h : h + 1]
-            top = jnp.maximum(old, jnp.max(scores, axis=1, keepdims=True))
+            scores = raw * COEF + bias
+            if h + 1 < GROUP:
+                raw = dot_t(keys, q_ref[:, (h + 1) * HD : (h + 2) * HD])
+            old = ml_in[0, h : h + 1, :]
+            top = jnp.maximum(old, jnp.max(scores, axis=0, keepdims=True))
             weights = jnp.exp2(scores - top)
             factor = jnp.exp2(old - top)
-            total = ml_old[:, GROUP + h : GROUP + h + 1] * factor + jnp.sum(
-                weights, axis=1, keepdims=True
+            total = ml_in[0, GROUP + h : GROUP + h + 1, :] * factor + jnp.sum(
+                weights, axis=0, keepdims=True
             )
-            acc = acc_in[:, cols] * factor + dot_n(weights.astype(jnp.bfloat16), values)
+            acc = acc_in[cols, :] * factor + dot_n(values, weights.astype(jnp.bfloat16))
             if last:
                 write(cols, acc, total)
             else:
-                outs[0][:, cols] = acc
-                ml = jnp.where(lane == h, top, ml)
-                ml = jnp.where(lane == GROUP + h, total, ml)
-        if not last:
-            outs[1][0] = ml
+                outs[0][cols, :] = acc
+                outs[1][0, h : h + 1, :] = top
+                outs[1][0, GROUP + h : GROUP + h + 1, :] = total
 
     @pl.when(jnp.logical_not(any_keys))
     def _():
         for h in range(GROUP):
             cols = slice(h * HD, (h + 1) * HD)
             if last:
-                write(cols, acc_in[:, cols], ml_in[0][:, GROUP + h : GROUP + h + 1])
+                write(cols, acc_in[cols, :], ml_in[0, GROUP + h : GROUP + h + 1, :])
             else:
-                outs[0][:, cols] = acc_in[:, cols]
+                outs[0][cols, :] = acc_in[cols, :]
         if not last:
-            outs[1][0] = ml_in[0]
+            outs[1][...] = ml_in[...]
 
 
 def decode_kernel(lens, q_ref, kv_ref, out_ref):
@@ -142,13 +136,13 @@
             in_specs=[pl.BlockSpec((rows, wide), lambda k, s: (0, k))]
             + [pl.BlockSpec((2, rows, HD), lambda k, s: (0, 0, k)) for _ in kvs],
             out_specs=[
-                pl.BlockSpec((rows, wide), lambda k, s: (0, k)),
-                pl.BlockSpec((1, rows, HD), lambda k, s: (k, 0, 0)),
+                pl.BlockSpec((wide, rows), lambda k, s: (k, 0)),
+                pl.BlockSpec((1, 2 * GROUP, rows), lambda k, s: (k, 0, 0)),
             ],
         ),
         out_shape=[
-            jax.ShapeDtypeStruct((rows, kv_local * wide), jnp.float32),
-            jax.ShapeDtypeStruct((kv_local, rows, HD), jnp.float32),
+            jax.ShapeDtypeStruct((kv_local * wide, rows), jnp.float32),
+            jax.ShapeDtypeStruct((kv_local, 2 * GROUP, rows), jnp.float32),
         ],
         cost_estimate=cost(rows, kv_local * GROUP, rows * len(kvs), rows * kv_local * wide * 6),
         name="local_stage",
@@ -160,12 +154,13 @@
     slots, tokens = kvs[0].shape[1], kvs[0].shape[2]
     kv_local = kvs[0].shape[3] // HD
     wide = GROUP * HD
-    acc_spec = pl.BlockSpec((rows, wide), lambda k, s: (0, k))
-    ml_spec = pl.BlockSpec((1, rows, HD), lambda k, s: (k, 0, 0))
+    q_spec = pl.BlockSpec((rows, wide), lambda k, s: (0, k))
+    acc_spec = pl.BlockSpec((wide, rows), lambda k, s: (k, 0))
+    ml_spec = pl.BlockSpec((1, 2 * GROUP, rows), lambda k, s: (k, 0, 0))
     parts = len(kvs)
     if last:
-        out_specs = [acc_spec]
-        out_shape = [jax.ShapeDtypeStruct(acc.shape, jnp.bfloat16)]
+        out_specs = [q_spec]
+        out_shape = [jax.ShapeDtypeStruct(q.shape, jnp.bfloat16)]
         aliases = {}
     else:
         out_specs = [acc_spec, ml_spec]

time: 120 us -> 91.6 us (0.76)
  Pallas kernels: 99.1 us -> 69.3 us
  waiting for transfers between devices: 3.74 us -> 6.98 us
  starting transfers between devices: 7.13 us -> 5.35 us
    pallas_call x4, Pallas kernels: 74.2 us -> 46.4 us  [run_pages(): pl.pallas_call(functools.partial(page_kernel, parts=parts, offset=offset,...]
    ppermute x8, waiting for transfers between devices: 3.74 us -> 6.98 us  [shift(): lax.ppermute(block, axis, [(i, (i + distance) % size) for i in range(size)])]
    pallas_call x1, Pallas kernels: 13.2 us -> 11.2 us  [run_local(): pl.pallas_call(functools.partial(local_kernel, parts=len(kvs)), grid_spec...]
    ppermute x8, starting transfers between devices: 7.13 us -> 5.35 us  [shift(): lax.ppermute(block, axis, [(i, (i + distance) % size) for i in range(size)])]
  transfers between devices with their start and end apart: 8 -> 8, of which waited for: 2 -> 4; matrix products, arithmetic and copies ran while one was open for 3% -> 4% of each run, Pallas kernels for 67% -> 63%
where the time goes in v1:
time: 91.6 us; the launch traced here: 91 us
  Pallas kernels  69.3 us (76%)
  waiting for transfers between devices  6.98 us (8%)
  local copies, waits for them, and re-layouts  6.39 us (7%)
  starting transfers between devices  5.35 us (6%)
  between operations  2.07 us (2%)
  other arithmetic  0.98 us (1%)
    pallas_call x4, Pallas kernels, run_pages(): pl.pallas_call(functools.partial(page_kernel, parts=parts, offset=offset,...  46.4 us
    pallas_call x1, Pallas kernels, run_decode(): pl.pallas_call(decode_kernel, grid_spec=pltpu.PrefetchScalarGridSpec(num_...  11.7 us
    pallas_call x1, Pallas kernels, run_local(): pl.pallas_call(functools.partial(local_kernel, parts=len(kvs)), grid_spec...  11.2 us
    ppermute x8, waiting for transfers between devices, shift(): lax.ppermute(block, axis, [(i, (i + distance) % size) for i in range(size)])  6.98 us
    ppermute x8, starting transfers between devices, shift(): lax.ppermute(block, axis, [(i, (i + distance) % size) for i in range(size)])  5.35 us
    unnamed x22, local copies, waits for them, and re-layouts  4.56 us
  transfers between devices with their start and end apart: 8, of which 4 were waited for; matrix products, arithmetic and copies ran while one was open for 4% of the time, Pallas kernels for 63%

profile of v1, /device:TPU:0, one launch (start us, length us, event | category | flops | bytes accessed | tf_op | source)
XLA Modules:
  0.0 91.0 jit_solution(4085785179681536941)
XLA Ops:
  0.6 0.0 copy-start.5
  0.7 1.7 %dynamic-slice_bitcast_fusion = (bf16[2,4,64,512]{3,2,1,0:T(8,128)(2,1)S(1)}, bf16[2,4,64,512]{3,2,1,0:T(8,128)(2,1)S(1)}, bf16[2,4,64,512]{3,2,1,0:T(8,128)(2,1)S(1)}, bf16[2,4,64,512]{3,2,1,0:T(8,128)(2,1)S(1)}) fusion(bf16[2,1,4,4,64,512]{5,4,3,2,1,0:T(8,128)(2,1)} %param.11, s32[]{:T(128)S(6)} %select_n.20, s32[]{:T(128)S(6)} %select_n.18, ...), kind=kLoop, calls=%fused_computation | loop fusion | bytes 4194320 | tf_op jit(solution)/shard_map/squeeze | solution.py:230
  2.4 0.0 copy-start.2
  2.4 4.1 %collective-permute-start.2 = (bf16[2,4,64,512]{3,2,1,0:T(8,128)(2,1)S(1)}, bf16[2,4,64,512]{3,2,1,0:T(8,128)(2,1)S(1)}, u32[]{:S(2)}, u32[]{:S(2)}) collective-permute-start(bf16[2,4,64,512]{3,2,1,0:T(8,128)(2,1)S(1)} %get-tuple-element.39), channel_id=1, source_target_pairs={{0,8},{4,12},{8,0},{12,4},{1,9},{5,13},{9,1},{13,5},{2,10},{6,14},... | collective-permute-start | bytes 1572872 | tf_op jit(solution)/shard_map/ppermute | solution.py:215
  6.6 0.0 collective-permute-start.3
  6.6 0.5 collective-permute-start.4
  7.1 0.1 iota_add_fusion
  7.2 0.2 select_reduce_fusion
  8.1 0.1 subtract_clamp_fusion
  8.2 0.1 min.12
  8.9 0.6 copy.22
  9.6 11.7 %decode_stage.1 = bf16[8,32,128]{2,1,0:T(8,128)(2,1)} custom-call(s32[8]{0:T(128)} %lens.1, bf16[8,32,128]{2,1,0:T(8,128)(2,1)} %bitcast.21, bf16[2,8,512,512]{3,2,1,0:T(8,128)(2,1)} %kv_ref.1), custom_call_target="tpu_custom_call" | custom-call | flops 67108864 | bytes 8388608 | tf_op jit(solution)/shard_map/decode_stage/pallas_call | solution.py:195
  21.2 1.5 %copy.21 = bf16[1,8,32,128]{3,1,2,0:T(8,128)(2,1)} copy(bf16[1,8,32,128]{3,2,1,0:T(8,128)(2,1)} %bitcast.20) | data formatting | bytes 131072
  22.7 0.6 pad_add_fusion.info
  23.3 0.0 collective-permute-done.4.refs_1_
  23.3 11.2 %local_stage.1 = (f32[4096,256]{1,0:T(8,128)}, f32[4,16,256]{2,1,0:T(8,128)}) custom-call(s32[36]{0:T(128)} %pad_add_fusion.info, bf16[256,4096]{1,0:T(8,128)(2,1)} %q_ref.9, bf16[2,256,512]{2,1,0:T(8,128)(2,1)} %refs_0_.1, bf16[2,256,512]{2,1,0:T(8,128)(2,1)} %collective-permute-done.4.refs_1_), custom_call_target="tpu_custom_call" | custom-call | flops 2147483648 | bytes 6291456 | tf_op jit(solution)/shard_map/local_stage/pallas_call | solution.py:131
  34.5 11.6 %page_stage.3 = (f32[4096,256]{1,0:T(8,128)}, f32[4,16,256]{2,1,0:T(8,128)}) custom-call(s32[36]{0:T(128)} %pad_add_fusion.info, bf16[256,4096]{1,0:T(8,128)(2,1)} %q_ref.9, bf16[2,4,64,512]{3,2,1,0:T(8,128)(2,1)} %copy-done.2, bf16[2,4,64,512]{3,2,1,0:T(8,128)(2,1)} %collective-permute-done.3.refs_1_, ...), custom_call_target="tpu_custom_call", output_to_operand_aliasing={{0}: (4, {}), {1}: (5, {})} | custom-call | flops 2147483648 | bytes 10485760 | tf_op jit(solution)/shard_map/page_stage/pallas_call | solution.py:172
  46.2 0.1 collective-permute-start.5
  46.2 0.1 collective-permute-start.1
  46.3 1.8 %collective-permute-done.5.refs_1_ = bf16[2,4,64,512]{3,2,1,0:T(8,128)(2,1)S(1)} collective-permute-done((bf16[2,4,64,512]{3,2,1,0:T(8,128)(2,1)S(1)}, bf16[2,4,64,512]{3,2,1,0:T(8,128)(2,1)S(1)}, u32[]{:S(2)}, u32[]{:S(2)}) %collective-permute-start.5) | collective-permute-done | bytes 524320 | tf_op jit(solution)/shard_map/ppermute | solution.py:215
  48.1 0.8 copy-done.9
  48.9 11.6 %page_stage.4 = (f32[4096,256]{1,0:T(8,128)}, f32[4,16,256]{2,1,0:T(8,128)}) custom-call(s32[36]{0:T(128)} %pad_add_fusion.info, bf16[256,4096]{1,0:T(8,128)(2,1)} %q_ref.9, bf16[2,4,64,512]{3,2,1,0:T(8,128)(2,1)} %copy-done.6, bf16[2,4,64,512]{3,2,1,0:T(8,128)(2,1)} %copy-done.9, ...), custom_call_target="tpu_custom_call", output_to_operand_aliasing={{0}: (4, {}), {1}: (5, {})} | custom-call | flops 2147483648 | bytes 10485760 | tf_op jit(solution)/shard_map/page_stage/pallas_call | solution.py:172
  60.5 1.8 %collective-permute-done.1.refs_0_ = bf16[2,4,64,512]{3,2,1,0:T(8,128)(2,1)S(1)} collective-permute-done((bf16[2,4,64,512]{3,2,1,0:T(8,128)(2,1)S(1)}, bf16[2,4,64,512]{3,2,1,0:T(8,128)(2,1)S(1)}, u32[]{:S(2)}, u32[]{:S(2)}) %collective-permute-start.1) | collective-permute-done | bytes 524320 | tf_op jit(solution)/shard_map/ppermute | solution.py:215
  62.4 0.4 collective-permute-start
  62.8 1.5 %collective-permute-done.6.refs_1_ = bf16[2,4,64,512]{3,2,1,0:T(8,128)(2,1)S(1)} collective-permute-done((bf16[2,4,64,512]{3,2,1,0:T(8,128)(2,1)S(1)}, bf16[2,4,64,512]{3,2,1,0:T(8,128)(2,1)S(1)}, u32[]{:S(2)}, u32[]{:S(2)}) %collective-permute-start.6) | collective-permute-done | bytes 524320 | tf_op jit(solution)/shard_map/ppermute | solution.py:215
  64.3 0.8 copy-done.8
  65.1 11.6 %page_stage.5 = (f32[4096,256]{1,0:T(8,128)}, f32[4,16,256]{2,1,0:T(8,128)}) custom-call(s32[36]{0:T(128)} %pad_add_fusion.info, bf16[256,4096]{1,0:T(8,128)(2,1)} %q_ref.9, bf16[2,4,64,512]{3,2,1,0:T(8,128)(2,1)} %copy-done.7, bf16[2,4,64,512]{3,2,1,0:T(8,128)(2,1)} %copy-done.8, ...), custom_call_target="tpu_custom_call", output_to_operand_aliasing={{0}: (4, {}), {1}: (5, {})} | custom-call | flops 2147483648 | bytes 10485760 | tf_op jit(solution)/shard_map/page_stage/pallas_call | solution.py:172
  76.7 0.0 collective-permute-done.refs_0_
  76.7 0.2 collective-permute-start.7
  76.9 1.8 %collective-permute-done.7.refs_1_ = bf16[2,4,64,512]{3,2,1,0:T(8,128)(2,1)S(1)} collective-permute-done((bf16[2,4,64,512]{3,2,1,0:T(8,128)(2,1)S(1)}, bf16[2,4,64,512]{3,2,1,0:T(8,128)(2,1)S(1)}, u32[]{:S(2)}, u32[]{:S(2)}) %collective-permute-start.7) | collective-permute-done | bytes 524320 | tf_op jit(solution)/shard_map/ppermute | solution.py:215
  78.7 0.8 copy-done.1
  79.5 11.6 %page_stage_last.1 = bf16[256,4096]{1,0:T(8,128)(2,1)} custom-call(s32[36]{0:T(128)} %pad_add_fusion.info, bf16[256,4096]{1,0:T(8,128)(2,1)} %q_ref.9, bf16[2,4,64,512]{3,2,1,0:T(8,128)(2,1)} %copy-done, bf16[2,4,64,512]{3,2,1,0:T(8,128)(2,1)} %copy-done.1, f32[4096,256]{1,0:T(8,128)} %get-tuple-element.33.refs_2_, f32[4,16,256]{2,1,0:T(8,128)} %get-tuple-element.34.refs_3_), custom_call_target="tpu_custom_call" | custom-call | flops 2147483648 | bytes 10485760 | tf_op jit(solution)/shard_map/page_stage_last/pallas_call | solution.py:172
  (22 shorter events, 0.1 us)
Async XLA Ops:
  0.6 6.0 %copy-start.5 = (bf16[2,256,512]{2,1,0:T(8,128)(2,1)S(1)}, bf16[2,256,512]{2,1,0:T(8,128)(2,1)}, u32[]{:S(2)}) copy-start(bf16[2,256,512]{2,1,0:T(8,128)(2,1)} %refs_0_.1) | copy-start | bytes 1572868
  0.6 6.5 %copy-start.4 = (s32[1,16]{1,0:T(1,128)S(1)}, s32[1,16]{1,0:T(1,128)}, u32[]{:S(2)}) copy-start(s32[1,16]{1,0:T(1,128)} %param.12) | copy-start | bytes 196
  0.7 8.3 %copy-start.3 = (bf16[8,4096]{1,0:T(8,128)(2,1)S(1)}, bf16[8,4096]{1,0:T(8,128)(2,1)}, u32[]{:S(2)}) copy-start(bf16[8,4096]{1,0:T(8,128)(2,1)} %param.15) | copy-start | bytes 196612
  2.4 18.8 %copy-start.2 = (bf16[2,4,64,512]{3,2,1,0:T(8,128)(2,1)}, bf16[2,4,64,512]{3,2,1,0:T(8,128)(2,1)S(1)}, u32[]{:S(2)}) copy-start(bf16[2,4,64,512]{3,2,1,0:T(8,128)(2,1)S(1)} %get-tuple-element.36.refs_0_) | copy-start | bytes 1572868
  2.4 43.7 %collective-permute-start.2 = (bf16[2,4,64,512]{3,2,1,0:T(8,128)(2,1)S(1)}, bf16[2,4,64,512]{3,2,1,0:T(8,128)(2,1)S(1)}, u32[]{:S(2)}, u32[]{:S(2)}) collective-permute-start(bf16[2,4,64,512]{3,2,1,0:T(8,128)(2,1)S(1)} %get-tuple-element.39), channel_id=1, source_target_pairs={{0,8},{4,12},{8,0},{12,4},{1,9},{5,13},{9,1},{13,5},{2,10},{6,14},... | collective-permute-start | bytes 1572872 | tf_op jit(solution)/shard_map/ppermute | solution.py:215
  6.6 28.0 %collective-permute-start.3 = (bf16[2,4,64,512]{3,2,1,0:T(8,128)(2,1)S(1)}, bf16[2,4,64,512]{3,2,1,0:T(8,128)(2,1)}, u32[]{:S(2)}, u32[]{:S(2)}) collective-permute-start(bf16[2,4,64,512]{3,2,1,0:T(8,128)(2,1)S(1)} %get-tuple-element.36.refs_0_), channel_id=1, source_target_pairs={{0,1},{1,0},{2,3},{3,2},{4,5},{5,4},{6,7},{7,6},{8,9},{9,8},{10,11... | collective-permute-start | bytes 1572872 | tf_op jit(solution)/shard_map/ppermute | solution.py:215
  6.6 16.7 %collective-permute-start.4 = (bf16[2,256,512]{2,1,0:T(8,128)(2,1)S(1)}, bf16[2,256,512]{2,1,0:T(8,128)(2,1)}, u32[]{:S(2)}, u32[]{:S(2)}) collective-permute-start(bf16[2,256,512]{2,1,0:T(8,128)(2,1)S(1)} %copy-done.5), channel_id=1, source_target_pairs={{0,1},{1,0},{2,3},{3,2},{4,5},{5,4},{6,7},{7,6},{8,9},{9,8},{10,11... | collective-permute-start | bytes 1572872 | tf_op jit(solution)/shard_map/ppermute | solution.py:215
  46.2 2.0 %copy-start.6 = (bf16[2,4,64,512]{3,2,1,0:T(8,128)(2,1)}, bf16[2,4,64,512]{3,2,1,0:T(8,128)(2,1)S(1)}, u32[]{:S(2)}) copy-start(bf16[2,4,64,512]{3,2,1,0:T(8,128)(2,1)S(1)} %collective-permute-done.2.refs_0_) | copy-start | bytes 1572868
  46.2 2.0 %collective-permute-start.5 = (bf16[2,4,64,512]{3,2,1,0:T(8,128)(2,1)S(1)}, bf16[2,4,64,512]{3,2,1,0:T(8,128)(2,1)S(1)}, u32[]{:S(2)}, u32[]{:S(2)}) collective-permute-start(bf16[2,4,64,512]{3,2,1,0:T(8,128)(2,1)S(1)} %collective-permute-done.2.refs_0_), channel_id=1, source_target_pairs={{0,1},{1,0},{2,3},{3,2},{4,5},{5,4},{6,7},{7,6},{8,9},{9,8},{10,11... | collective-permute-start | bytes 1572872 | tf_op jit(solution)/shard_map/ppermute | solution.py:215
  46.2 16.1 %collective-permute-start.1 = (bf16[2,4,64,512]{3,2,1,0:T(8,128)(2,1)S(1)}, bf16[2,4,64,512]{3,2,1,0:T(8,128)(2,1)S(1)}, u32[]{:S(2)}, u32[]{:S(2)}) collective-permute-start(bf16[2,4,64,512]{3,2,1,0:T(8,128)(2,1)S(1)} %get-tuple-element.37), channel_id=1, source_target_pairs={{0,4},{4,8},{8,12},{12,0},{1,5},{5,9},{9,13},{13,1},{2,6},{6,10},{... | collective-permute-start | bytes 1572872 | tf_op jit(solution)/shard_map/ppermute | solution.py:215
  48.1 0.8 copy-start.9
  62.4 1.9 %copy-start.7 = (bf16[2,4,64,512]{3,2,1,0:T(8,128)(2,1)}, bf16[2,4,64,512]{3,2,1,0:T(8,128)(2,1)S(1)}, u32[]{:S(2)}) copy-start(bf16[2,4,64,512]{3,2,1,0:T(8,128)(2,1)S(1)} %collective-permute-done.1.refs_0_) | copy-start | bytes 1572868
  62.4 1.9 %collective-permute-start.6 = (bf16[2,4,64,512]{3,2,1,0:T(8,128)(2,1)S(1)}, bf16[2,4,64,512]{3,2,1,0:T(8,128)(2,1)S(1)}, u32[]{:S(2)}, u32[]{:S(2)}) collective-permute-start(bf16[2,4,64,512]{3,2,1,0:T(8,128)(2,1)S(1)} %collective-permute-done.1.refs_0_), channel_id=1, source_target_pairs={{0,1},{1,0},{2,3},{3,2},{4,5},{5,4},{6,7},{7,6},{8,9},{9,8},{10,11... | collective-permute-start | bytes 1572872 | tf_op jit(solution)/shard_map/ppermute | solution.py:215
  62.4 14.3 %collective-permute-start = (bf16[2,4,64,512]{3,2,1,0:T(8,128)(2,1)S(1)}, bf16[2,4,64,512]{3,2,1,0:T(8,128)(2,1)S(1)}, u32[]{:S(2)}, u32[]{:S(2)}) collective-permute-start(bf16[2,4,64,512]{3,2,1,0:T(8,128)(2,1)S(1)} %get-tuple-element.38), channel_id=1, source_target_pairs={{0,12},{4,0},{8,4},{12,8},{1,13},{5,1},{9,5},{13,9},{2,14},{6,2},{... | collective-permute-start | bytes 1572872 | tf_op jit(solution)/shard_map/ppermute | solution.py:215
  64.3 0.8 copy-start.8
  76.7 2.0 %copy-start = (bf16[2,4,64,512]{3,2,1,0:T(8,128)(2,1)}, bf16[2,4,64,512]{3,2,1,0:T(8,128)(2,1)S(1)}, u32[]{:S(2)}) copy-start(bf16[2,4,64,512]{3,2,1,0:T(8,128)(2,1)S(1)} %collective-permute-done.refs_0_) | copy-start | bytes 1572868
  76.7 2.0 %collective-permute-start.7 = (bf16[2,4,64,512]{3,2,1,0:T(8,128)(2,1)S(1)}, bf16[2,4,64,512]{3,2,1,0:T(8,128)(2,1)S(1)}, u32[]{:S(2)}, u32[]{:S(2)}) collective-permute-start(bf16[2,4,64,512]{3,2,1,0:T(8,128)(2,1)S(1)} %collective-permute-done.refs_0_), channel_id=1, source_target_pairs={{0,1},{1,0},{2,3},{3,2},{4,5},{5,4},{6,7},{7,6},{8,9},{9,8},{10,11... | collective-permute-start | bytes 1572872 | tf_op jit(solution)/shard_map/ppermute | solution.py:215
  78.7 0.8 copy-start.1
